TPU v7x, 32 devices: a whole 2x2x4 slice. The times are simulated.
32 devices in a mesh: atoms: 8 (over z, y), modes: 4 (over x, core).
Axes of the slice: x: 2, y: 2, z: 4, core: 2. Of those that a mesh axis runs over, the one named last changes fastest.
Arguments:
- eigvec: bfloat16 [3072, 2048], P('atoms', 'modes'), may hold values from -6 to 6
- operator_blocks: bfloat16 [24, 8, 128, 128], P('atoms'), may hold values from -0.0034179688 to 0.0034179688
- column_blocks: int32 [24, 8], P('atoms'), may hold values from 0 to 23, as said below
- block_mask: int32 [24, 8], P('atoms'), may hold values 0 or 1
- spectrum: float32 [3072], replicated, may hold values from 0.5 to 20
- mode_index: int32 [2048], replicated, may hold values from 0 to 3071
- linewidth: float32 [2048], replicated, may hold values from 0.05 to 1
Outputs:
- flux_tiles: float32 [2048, 2048], P('modes', 'atoms')
- diffusivity: float32 [2048], P('modes')
Inputs may be any that keep to these rules, and one draw needn't show every extreme that they name: `column_blocks`: the 8 column blocks of row block r are distinct and lie within 4 blocks of r, counted around the cycle of 24 blocks.
All inputs are finite; a program needn't handle non-finite values. No bound on the sum of `block_mask` on one device may be relied on, other than what follows from the above.
Results may differ from a plain program's by a relative error of at most 0.0058.
Values may be sent and summed in bfloat16 or wider, within the bound.
No kernel may reach another device: no remote copies, remote signals or barrier semaphores. Data moves between devices by JAX's collectives and lax.ppermute only.
A program may use at most 64 MiB of HBM per device.

v0:
```python
import jax
import jax.numpy as jnp
from jax import lax
from jax.sharding import PartitionSpec as P

REACH = 4


def with_halo(block, sides, width):
    for axis, dim in sides:
        count = lax.axis_size(axis)
        forward = [(i, i + 1) for i in range(count - 1)]
        forward.append((count - 1, 0))
        backward = [(target, source) for source, target in forward]
        low = lax.ppermute(
            lax.slice_in_dim(block, block.shape[dim] - width, None, axis=dim), axis, forward
        )
        high = lax.ppermute(lax.slice_in_dim(block, 0, width, axis=dim), axis, backward)
        block = jnp.concatenate([low, block, high], axis=dim)
    return block


def from_behind(value, axis, by):
    devices = lax.axis_size(axis)
    return lax.ppermute(value, axis, [(i, (i + by) % devices) for i in range(devices)])


def pair_weight(row_freq, col_freq, row_width, col_width):
    freq_sum = row_freq[:, None] + col_freq[None, :]
    spacing = row_freq[:, None] - col_freq[None, :]
    mean_width = 0.5 * (row_width[:, None] + col_width[None, :])
    factor = freq_sum * freq_sum / (4.0 * row_freq[:, None] * col_freq[None, :])
    return factor * mean_width / (spacing * spacing + mean_width * mean_width)


def body(eigvec, operator_blocks, column_blocks, block_mask, spectrum, mode_index, linewidth):
    block_width = operator_blocks.shape[2]
    local_blocks = operator_blocks.shape[0]
    own_modes = eigvec.shape[1]
    atom_count = lax.axis_size("atoms")
    atom_rank = lax.axis_index("atoms")
    group_rank = lax.axis_index("modes")
    total_blocks = local_blocks * atom_count
    near_blocks = min(REACH, local_blocks)
    extra_blocks = REACH - near_blocks
    extended = with_halo(eigvec, (("atoms", 0),), near_blocks * block_width)
    far_pieces = []
    slab_rows = eigvec.shape[0]
    for distance, far_rows in (
        (2, eigvec[slab_rows - extra_blocks * block_width :]),
        (-2, eigvec[: extra_blocks * block_width]),
    ):
        far_pieces.append(from_behind(far_rows, "atoms", distance))
    extended = jnp.concatenate([far_pieces[0], extended, far_pieces[1]], axis=0)
    ext_blocks = extended.reshape(-1, block_width, own_modes)
    offsets = (column_blocks - atom_rank * local_blocks + REACH) % total_blocks
    picked = ext_blocks[offsets]
    masked = jnp.where(
        block_mask[:, :, None, None] > 0, operator_blocks, jnp.zeros((), operator_blocks.dtype)
    )
    product = jnp.einsum("bsij,bsjm->bim", masked, picked, preferred_element_type=jnp.float32)
    velocity = product.reshape(-1, own_modes).astype(jnp.bfloat16)
    contract = (((0,), (0,)), ((), ()))
    stacked = jnp.stack((eigvec, velocity))
    piece = lax.all_gather(stacked, "modes", axis=2, tiled=True)
    direct = lax.dot_general(eigvec, piece[1], contract, preferred_element_type=jnp.float32)
    mirror = lax.dot_general(velocity, piece[0], contract, preferred_element_type=jnp.float32)
    partial_flux = direct - mirror
    frequency = spectrum[mode_index]
    mode_total = frequency.shape[0]
    row_freq = lax.dynamic_slice_in_dim(frequency, group_rank * own_modes, own_modes)
    row_width = lax.dynamic_slice_in_dim(linewidth, group_rank * own_modes, own_modes)
    flux_tiles = lax.psum_scatter(partial_flux, "atoms", scatter_dimension=1, tiled=True)
    share_cols = flux_tiles.shape[1]
    col_freq = lax.dynamic_slice_in_dim(frequency, atom_rank * share_cols, share_cols)
    col_width = lax.dynamic_slice_in_dim(linewidth, atom_rank * share_cols, share_cols)
    weight = pair_weight(row_freq, col_freq, row_width, col_width)
    partial_sums = jnp.sum(weight * flux_tiles * flux_tiles, axis=1)
    diffusivity = lax.psum(partial_sums, "atoms") / mode_total
    return (flux_tiles, diffusivity)


def solution(mesh):
    return jax.shard_map(
        body,
        mesh=mesh,
        in_specs=(
            P("atoms", "modes"),
            P("atoms", None, None, None),
            P("atoms", None),
            P("atoms", None),
            P(),
            P(),
            P(),
        ),
        out_specs=(P("modes", "atoms"), P("modes")),
        check_vma=False,
    )
```

profile of v0, /device:TPU:0, one launch (start us, length us, event | category | flops | bytes accessed | tf_op | source)
XLA Modules:
  0.0 190.7 jit_solution(3013276178611091838)
XLA Ops:
  7.2 0.0 all-gather.2.cloned.1.call-start
  7.2 3.0 %collective-permute-start.1 = (bf16[384,512]{1,0:T(8,128)(2,1)}, bf16[384,512]{1,0:T(8,128)(2,1)S(1)}, u32[]{:S(2)}, u32[]{:S(2)}) collective-permute-start(bf16[384,512]{1,0:T(8,128)(2,1)} %param.7), channel_id=1, source_target_pairs={{0,4},{4,8},{8,12},{12,16},{16,20},{20,24},{24,28},{28,0},{1,5},{5... | collective-permute-start | bytes 1179656 | tf_op jit(solution)/shard_map/ppermute | solution.py:15
  10.3 3.1 %collective-permute-start.2 = (bf16[384,512]{1,0:T(8,128)(2,1)}, bf16[384,512]{1,0:T(8,128)(2,1)S(1)}, u32[]{:S(2)}, u32[]{:S(2)}) collective-permute-start(bf16[384,512]{1,0:T(8,128)(2,1)} %param.7), channel_id=1, source_target_pairs={{4,0},{8,4},{12,8},{16,12},{20,16},{24,20},{28,24},{0,28},{5,1},{9... | collective-permute-start | bytes 1179656 | tf_op jit(solution)/shard_map/ppermute | solution.py:18
  13.4 1.0 fusion.8
  14.4 0.1 collective-permute-start
  14.4 3.8 %collective-permute-start.3 = (bf16[128,512]{1,0:T(8,128)(2,1)S(1)}, bf16[128,512]{1,0:T(8,128)(2,1)S(1)}, u32[]{:S(2)}, u32[]{:S(2)}) collective-permute-start(bf16[128,512]{1,0:T(8,128)(2,1)S(1)} %get-tuple-element.8), channel_id=1, source_target_pairs={{0,24},{4,28},{8,0},{12,4},{16,8},{20,12},{24,16},{28,20},{1,25},{... | collective-permute-start | bytes 393224 | tf_op jit(solution)/shard_map/ppermute | solution.py:25
  18.3 0.7 compare_select_fusion.1
  19.0 1.2 broadcast_compare_fusion
  20.2 0.1 reshape.31
  20.2 8.0 %collective-permute-done = bf16[128,512]{1,0:T(8,128)(2,1)S(1)} collective-permute-done((bf16[128,512]{1,0:T(8,128)(2,1)S(1)}, bf16[128,512]{1,0:T(8,128)(2,1)S(1)}, u32[]{:S(2)}, u32[]{:S(2)}) %collective-permute-start) | collective-permute-done | bytes 131104 | tf_op jit(solution)/shard_map/ppermute | solution.py:25
  28.4 1.1 collective-permute-done.2
  29.6 1.1 copy-done.1
  30.7 2.1 %gather_fusion = bf16[24,128,512]{2,1,0:T(8,128)(2,1)S(1)} fusion(bf16[11,128,512]{2,1,0:T(8,128)(2,1)} %bitcast.22, s32[1024]{0:T(1024)S(1)} %pad_clamp_fusion), kind=kCustom, calls=%fused_computation | custom fusion | bytes 6291552 | tf_op jit(solution)/shard_map/gather | solution.py:57
  32.8 1.8 fusion.1
  34.6 0.7 copy-done.4
  35.3 1.0 pad_maximum_fusion
  36.3 0.0 all-gather.2.cloned.1.call-update
  36.3 0.0 reduce-scatter.2.cloned.1.call-start
  36.4 28.7 %all-gather.2.cloned.1.call-done = bf16[2,384,2048]{2,1,0:T(8,128)(2,1)} async-done(((bf16[2,384,512]{2,1,0:T(8,128)(2,1)}), bf16[2,384,2048]{2,1,0:T(8,128)(2,1)}) %all-gather.2.cloned.1.call-update) | async-done | bytes 3145744 | tf_op jit(solution)/shard_map/all_gather | solution.py:65
  65.1 2.9 %fusion = f32[2048,512]{1,0:T(8,128)S(1)} fusion(bf16[384,512]{1,0:T(8,128)(2,1)S(1)} %copy-done.2, bf16[2,384,2048]{2,1,0:T(8,128)(2,1)} %all-gather.2.cloned.1.call-done), kind=kOutput, calls=%fused_computation.5 | convolution fusion | flops 805306368 | bytes 6160384 | tf_op jit(solution)/shard_map/dot_general | solution.py:66
  68.0 3.3 %bitcast_subtract_fusion = f32[512,2048]{0,1:T(8,128)} fusion(f32[2048,512]{1,0:T(8,128)S(1)} %fusion, bf16[384,512]{1,0:T(8,128)(2,1)S(1)} %bitcast.25, bf16[2,384,2048]{2,1,0:T(8,128)(2,1)S(1)} %copy-done.3), kind=kOutput, calls=%fused_computation.2 | convolution fusion | flops 806354944 | bytes 10354688 | tf_op jit(solution)/shard_map/dot_general | solution.py:67
  71.3 0.7 copy-done.6
  71.9 11.8 %gather_fusion.1 = f32[2048]{0:T(1024)S(1)} fusion(f32[3072]{0:T(1024)S(1)} %copy-done, s32[2048]{0:T(1024)S(1)} %fusion.6), kind=kCustom, calls=%fused_computation.1 | custom fusion | bytes 24576 | tf_op jit(solution)/shard_map/gather | solution.py:69
  83.7 0.1 dynamic_slice.13
  83.8 0.8 dynamic_slice.15
  84.6 0.8 dynamic_slice.14
  85.3 0.1 broadcast_multiply_fusion.1
  85.4 74.3 %reduce-scatter.2.cloned.1.call-done = f32[512,256]{0,1:T(8,128)} async-done(((f32[512,2048]{0,1:T(8,128)}), f32[512,256]{0,1:T(8,128)}) %reduce-scatter.2.cloned.1.call-update) | async-done | bytes 524304 | tf_op jit(solution)/shard_map/reduce_scatter | solution.py:73
  159.7 1.4 fusion.4
  161.2 20.1 %psum.7 = f32[512]{0:T(512)S(1)} all-reduce(f32[512]{0:T(512)S(1)} %fusion.4), channel_id=1, replica_groups=mesh['atoms'=8,'modes'=4] {'atoms'}, use_global_device_ids=true, to_apply=%region_2.3 | all-reduce | flops 512 | bytes 4096 | tf_op jit(solution)/shard_map/psum | solution.py:79
  181.2 0.6 broadcast_multiply_fusion
  181.8 2.0 %copy.12 = f32[512,256]{1,0:T(8,128)} copy(f32[512,256]{0,1:T(8,128)} %reduce-scatter.2.cloned.1.call-done) | data formatting | bytes 1048576
  (21 shorter events, 0.2 us)
Async XLA Ops:
  7.2 64.8 %copy-start = (f32[3072]{0:T(1024)S(1)}, f32[3072]{0:T(1024)}, u32[]{:S(2)}) copy-start(f32[3072]{0:T(1024)} %param.11) | copy-start | bytes 36868
  7.2 21.2 %copy-start.2 = (bf16[384,512]{1,0:T(8,128)(2,1)S(1)}, bf16[384,512]{1,0:T(8,128)(2,1)}, u32[]{:S(2)}) copy-start(bf16[384,512]{1,0:T(8,128)(2,1)} %param.7) | copy-start | bytes 1179652
  7.2 57.9 %all-gather.2.cloned.1.call-start = ((), (), s32[]{:S(2)}) async-start(), calls=%async_computation.1 | async-start | bytes 3932160 | tf_op jit(solution)/shard_map/all_gather | solution.py:65
  7.2 21.1 %collective-permute-start.1 = (bf16[384,512]{1,0:T(8,128)(2,1)}, bf16[384,512]{1,0:T(8,128)(2,1)S(1)}, u32[]{:S(2)}, u32[]{:S(2)}) collective-permute-start(bf16[384,512]{1,0:T(8,128)(2,1)} %param.7), channel_id=1, source_target_pairs={{0,4},{4,8},{8,12},{12,16},{16,20},{20,24},{24,28},{28,0},{1,5},{5... | collective-permute-start | bytes 1179656 | tf_op jit(solution)/shard_map/ppermute | solution.py:15
  10.3 19.2 %collective-permute-start.2 = (bf16[384,512]{1,0:T(8,128)(2,1)}, bf16[384,512]{1,0:T(8,128)(2,1)S(1)}, u32[]{:S(2)}, u32[]{:S(2)}) collective-permute-start(bf16[384,512]{1,0:T(8,128)(2,1)} %param.7), channel_id=1, source_target_pairs={{4,0},{8,4},{12,8},{16,12},{20,16},{24,20},{28,24},{0,28},{5,1},{9... | collective-permute-start | bytes 1179656 | tf_op jit(solution)/shard_map/ppermute | solution.py:18
  14.4 13.9 %collective-permute-start = (bf16[128,512]{1,0:T(8,128)(2,1)S(1)}, bf16[128,512]{1,0:T(8,128)(2,1)S(1)}, u32[]{:S(2)}, u32[]{:S(2)}) collective-permute-start(bf16[128,512]{1,0:T(8,128)(2,1)S(1)} %get-tuple-element.9), channel_id=1, source_target_pairs={{0,8},{4,12},{8,16},{12,20},{16,24},{20,28},{24,0},{28,4},{1,9},{5... | collective-permute-start | bytes 393224 | tf_op jit(solution)/shard_map/ppermute | solution.py:25
  14.4 15.1 %collective-permute-start.3 = (bf16[128,512]{1,0:T(8,128)(2,1)S(1)}, bf16[128,512]{1,0:T(8,128)(2,1)S(1)}, u32[]{:S(2)}, u32[]{:S(2)}) collective-permute-start(bf16[128,512]{1,0:T(8,128)(2,1)S(1)} %get-tuple-element.8), channel_id=1, source_target_pairs={{0,24},{4,28},{8,0},{12,4},{16,8},{20,12},{24,16},{28,20},{1,25},{... | collective-permute-start | bytes 393224 | tf_op jit(solution)/shard_map/ppermute | solution.py:25
  29.6 1.1 copy-start.1
  34.6 0.7 copy-start.4
  36.3 31.6 %copy-start.5 = (bf16[3,128,512]{2,1,0:T(8,128)(2,1)S(1)}, bf16[3,128,512]{2,1,0:T(8,128)(2,1)}, u32[]{:S(2)}) copy-start(bf16[3,128,512]{2,1,0:T(8,128)(2,1)} %copy-done.4) | copy-start | bytes 1179652
  36.3 123.4 %reduce-scatter.2.cloned.1.call-start = ((), (), s32[]{:S(2)}) async-start(), calls=%async_computation.2 | async-start | bytes 4718592 | tf_op jit(solution)/shard_map/reduce_scatter | solution.py:73
  65.1 2.9 %copy-start.3 = (bf16[2,384,2048]{2,1,0:T(8,128)(2,1)S(1)}, bf16[2,384,2048]{2,1,0:T(8,128)(2,1)}, u32[]{:S(2)}) copy-start(bf16[2,384,2048]{2,1,0:T(8,128)(2,1)} %all-gather.2.cloned.1.call-done) | copy-start | bytes 9437188
  71.2 0.7 copy-start.6
Sparse Core Ops, SparseCore 0:
  36.4 28.6 all-gather.1
  71.4 88.2 reduce-scatter.1
where the time goes:
time: 191 us
  waiting for transfers between devices  112 us (59%)
  local copies, waits for them, and re-layouts  21.3 us (11%)
  blocking collectives  20.1 us (11%)
  between operations  14.2 us (7%)
  starting transfers between devices  10.1 us (5%)
  matrix products  7.9 us (4%)
  other arithmetic  4.96 us (3%)
    reduce_scatter x1, waiting for transfers between devices, body(): lax.psum_scatter(partial_flux, 'atoms', scatter_dimension=1, tiled=True)  74.3 us
    all_gather x1, waiting for transfers between devices, body(): piece = lax.all_gather(stacked, 'modes', axis=2, tiled=True)  28.7 us
    psum x1, blocking collectives, body(): diffusivity = lax.psum(partial_sums, 'atoms') / mode_total  20.1 us
    gather x1, local copies, waits for them, and re-layouts, body(): frequency = spectrum[mode_index]  11.8 us
    ppermute x2, waiting for transfers between devices, from_behind(): lax.ppermute(value, axis, [(i, (i + by) % devices) for i in range(devices)])  8.03 us
    unnamed x19, local copies, waits for them, and re-layouts  4.68 us
    ppermute x2, starting transfers between devices, from_behind(): lax.ppermute(value, axis, [(i, (i + by) % devices) for i in range(devices)])  3.87 us
  transfers between devices with their start and end apart: 6, of which 4 were waited for; matrix products, arithmetic and copies ran while one was open for 9% of the time, Pallas kernels for 0%

commit v1 on v0

--- a/solution.py
+++ b/solution.py
@@ -62,7 +62,7 @@
     velocity = product.reshape(-1, own_modes).astype(jnp.bfloat16)
     contract = (((0,), (0,)), ((), ()))
     stacked = jnp.stack((eigvec, velocity))
-    piece = lax.all_gather(stacked, "modes", axis=2, tiled=True)
+    piece = jnp.concatenate(lax.all_gather(stacked, "modes"), axis=2)
     direct = lax.dot_general(eigvec, piece[1], contract, preferred_element_type=jnp.float32)
     mirror = lax.dot_general(velocity, piece[0], contract, preferred_element_type=jnp.float32)
     partial_flux = direct - mirror

time: 191 us -> 200 us (1.047)
  local copies, waits for them, and re-layouts: 21.3 us -> 27.5 us
  matrix products: 7.9 us -> 10.3 us
    slice x0 -> x3, local copies, waits for them, and re-layouts: none -> 6.09 us  [the longest x2 4.2 us: body(): piece[0]]
    dot_general x1, matrix products: 3.27 us -> 5.38 us  [body(): lax.dot_general(velocity, piece[0], contract, preferred_element_type=jnp....]
    unnamed x19 -> x17, local copies, waits for them, and re-layouts: 4.68 us -> 4.8 us
  transfers between devices with their start and end apart: 6 -> 6, of which waited for: 4 -> 4; matrix products, arithmetic and copies ran while one was open for 9% -> 8% of each run, Pallas kernels for 0% -> 0%
where the time goes in v1:
time: 200 us; the launch traced here: 199 us
  waiting for transfers between devices  112 us (56%)
  local copies, waits for them, and re-layouts  27.5 us (14%)
  blocking collectives  20.1 us (10%)
  between operations  14.2 us (7%)
  matrix products  10.3 us (5%)
  starting transfers between devices  10.1 us (5%)
  other arithmetic  4.96 us (2%)
    reduce_scatter x1, waiting for transfers between devices, body(): lax.psum_scatter(partial_flux, 'atoms', scatter_dimension=1, tiled=True)  74.3 us
    all_gather x1, waiting for transfers between devices, body(): piece = jnp.concatenate(lax.all_gather(stacked, 'modes'), axis=2)  28.7 us
    psum x1, blocking collectives, body(): diffusivity = lax.psum(partial_sums, 'atoms') / mode_total  20.1 us
    gather x1, local copies, waits for them, and re-layouts, body(): frequency = spectrum[mode_index]  11.8 us
    ppermute x2, waiting for transfers between devices, from_behind(): lax.ppermute(value, axis, [(i, (i + by) % devices) for i in range(devices)])  8.03 us
    dot_general x1, matrix products, body(): lax.dot_general(velocity, piece[0], contract, preferred_element_type=jnp....  5.38 us
    unnamed x17, local copies, waits for them, and re-layouts  4.8 us
    slice x2, local copies, waits for them, and re-layouts, body(): piece[0]  4.2 us
  transfers between devices with their start and end apart: 6, of which 4 were waited for; matrix products, arithmetic and copies ran while one was open for 8% of the time, Pallas kernels for 0%

profile of v1, /device:TPU:0, one launch (start us, length us, event | category | flops | bytes accessed | tf_op | source)
XLA Modules:
  0.0 199.3 jit_solution(713083046490102267)
XLA Ops:
  7.2 3.0 %collective-permute-start.1 = (bf16[384,512]{1,0:T(8,128)(2,1)}, bf16[384,512]{1,0:T(8,128)(2,1)S(1)}, u32[]{:S(2)}, u32[]{:S(2)}) collective-permute-start(bf16[384,512]{1,0:T(8,128)(2,1)} %param.7), channel_id=1, source_target_pairs={{0,4},{4,8},{8,12},{12,16},{16,20},{20,24},{24,28},{28,0},{1,5},{5... | collective-permute-start | bytes 1179656 | tf_op jit(solution)/shard_map/ppermute | solution.py:15
  10.3 3.1 %collective-permute-start.2 = (bf16[384,512]{1,0:T(8,128)(2,1)}, bf16[384,512]{1,0:T(8,128)(2,1)S(1)}, u32[]{:S(2)}, u32[]{:S(2)}) collective-permute-start(bf16[384,512]{1,0:T(8,128)(2,1)} %param.7), channel_id=1, source_target_pairs={{4,0},{8,4},{12,8},{16,12},{20,16},{24,20},{28,24},{0,28},{5,1},{9... | collective-permute-start | bytes 1179656 | tf_op jit(solution)/shard_map/ppermute | solution.py:18
  13.4 1.0 fusion.8
  14.4 3.8 %collective-permute-start.3 = (bf16[128,512]{1,0:T(8,128)(2,1)S(1)}, bf16[128,512]{1,0:T(8,128)(2,1)S(1)}, u32[]{:S(2)}, u32[]{:S(2)}) collective-permute-start(bf16[128,512]{1,0:T(8,128)(2,1)S(1)} %get-tuple-element.14), channel_id=1, source_target_pairs={{0,24},{4,28},{8,0},{12,4},{16,8},{20,12},{24,16},{28,20},{1,25},{... | collective-permute-start | bytes 393224 | tf_op jit(solution)/shard_map/ppermute | solution.py:25
  18.3 0.7 compare_select_fusion.1
  19.0 1.2 broadcast_compare_fusion
  20.2 0.1 reshape.40
  20.2 8.0 %collective-permute-done = bf16[128,512]{1,0:T(8,128)(2,1)S(1)} collective-permute-done((bf16[128,512]{1,0:T(8,128)(2,1)S(1)}, bf16[128,512]{1,0:T(8,128)(2,1)S(1)}, u32[]{:S(2)}, u32[]{:S(2)}) %collective-permute-start) | collective-permute-done | bytes 131104 | tf_op jit(solution)/shard_map/ppermute | solution.py:25
  28.4 1.1 collective-permute-done.2
  29.6 1.1 copy-done.1
  30.7 2.1 %gather_fusion = bf16[24,128,512]{2,1,0:T(8,128)(2,1)S(1)} fusion(bf16[11,128,512]{2,1,0:T(8,128)(2,1)} %bitcast.24, s32[1024]{0:T(1024)S(1)} %pad_clamp_fusion), kind=kCustom, calls=%fused_computation | custom fusion | bytes 6291552 | tf_op jit(solution)/shard_map/gather | solution.py:57
  32.8 1.8 fusion
  34.6 0.7 copy-done.3
  35.3 1.0 pad_maximum_fusion
  36.4 28.7 %all-gather.3.cloned.1.call-done = bf16[8,384,512]{2,1,0:T(8,128)(2,1)} async-done(((bf16[2,384,512]{2,1,0:T(8,128)(2,1)}), bf16[8,384,512]{2,1,0:T(8,128)(2,1)}) %all-gather.3.cloned.1.call-update) | async-done | bytes 3145744 | tf_op jit(solution)/shard_map/all_gather | solution.py:65
  65.1 3.3 %fusion.7 = (bf16[1,384,4,512]{3,1,0,2:T(8,128)(2,1)S(1)}, bf16[1,384,4,512]{3,1,0,2:T(8,128)(2,1)}) fusion(bf16[2,384,4,512]{3,1,0,2:T(8,128)(2,1)} %bitcast.29), kind=kLoop, calls=%fused_computation.26 | loop fusion | bytes 6291456 | tf_op jit(solution)/shard_map/slice | solution.py:67
  68.4 1.9 copy.17
  70.3 3.2 %fusion.9 = f32[2048,512]{1,0:T(8,128)} fusion(bf16[384,2048]{0,1:T(8,128)(2,1)S(1)} %bitcast.23, bf16[384,512]{1,0:T(8,128)(2,1)S(1)} %copy-done.2), kind=kOutput, calls=%fused_computation.28 | convolution fusion | flops 805306368 | bytes 6160384 | tf_op jit(solution)/shard_map/dot_general | solution.py:66
  73.5 0.9 copy.18
  74.4 0.1 copy-done.4
  74.5 5.4 %bitcast_subtract_fusion = f32[512,2048]{0,1:T(8,128)} fusion(f32[2048,512]{1,0:T(8,128)} %fusion.9, bf16[384,2048]{0,1:T(8,128)(2,1)S(1)} %bitcast.25, bf16[384,512]{1,0:T(8,128)(2,1)S(1)} %bitcast.28), kind=kOutput, calls=%fused_computation.2 | convolution fusion | flops 806354944 | bytes 10354688 | tf_op jit(solution)/shard_map/dot_general | solution.py:67
  79.9 0.7 copy-done.5
  80.6 11.8 %gather_fusion.1 = f32[2048]{0:T(1024)S(1)} fusion(f32[3072]{0:T(1024)S(1)} %copy-done, s32[2048]{0:T(1024)S(1)} %fusion.5), kind=kCustom, calls=%fused_computation.1 | custom fusion | bytes 24576 | tf_op jit(solution)/shard_map/gather | solution.py:69
  92.4 0.1 dynamic_slice.13
  92.5 0.8 dynamic_slice.15
  93.2 0.8 dynamic_slice.14
  94.0 0.1 broadcast_multiply_fusion.1
  94.1 74.3 %reduce-scatter.2.cloned.1.call-done = f32[512,256]{0,1:T(8,128)} async-done(((f32[512,2048]{0,1:T(8,128)}), f32[512,256]{0,1:T(8,128)}) %reduce-scatter.2.cloned.1.call-update) | async-done | bytes 524304 | tf_op jit(solution)/shard_map/reduce_scatter | solution.py:73
  168.4 1.4 fusion.3
  169.8 20.1 %psum.7 = f32[512]{0:T(512)S(1)} all-reduce(f32[512]{0:T(512)S(1)} %fusion.3), channel_id=1, replica_groups=mesh['atoms'=8,'modes'=4] {'atoms'}, use_global_device_ids=true, to_apply=%region_2.3 | all-reduce | flops 512 | bytes 4096 | tf_op jit(solution)/shard_map/psum | solution.py:79
  189.9 0.6 broadcast_multiply_fusion
  190.5 2.0 %copy.20 = f32[512,256]{1,0:T(8,128)} copy(f32[512,256]{0,1:T(8,128)} %reduce-scatter.2.cloned.1.call-done) | data formatting | bytes 1048576
  (22 shorter events, 0.3 us)
Async XLA Ops:
  7.2 73.4 %copy-start = (f32[3072]{0:T(1024)S(1)}, f32[3072]{0:T(1024)}, u32[]{:S(2)}) copy-start(f32[3072]{0:T(1024)} %param.11) | copy-start | bytes 36868
  7.2 21.2 %copy-start.2 = (bf16[384,512]{1,0:T(8,128)(2,1)S(1)}, bf16[384,512]{1,0:T(8,128)(2,1)}, u32[]{:S(2)}) copy-start(bf16[384,512]{1,0:T(8,128)(2,1)} %param.7) | copy-start | bytes 1179652
  7.2 57.9 %all-gather.3.cloned.1.call-start = ((), (), s32[]{:S(2)}) async-start(), calls=%async_computation.2 | async-start | bytes 3932160 | tf_op jit(solution)/shard_map/all_gather | solution.py:65
  7.2 21.1 %collective-permute-start.1 = (bf16[384,512]{1,0:T(8,128)(2,1)}, bf16[384,512]{1,0:T(8,128)(2,1)S(1)}, u32[]{:S(2)}, u32[]{:S(2)}) collective-permute-start(bf16[384,512]{1,0:T(8,128)(2,1)} %param.7), channel_id=1, source_target_pairs={{0,4},{4,8},{8,12},{12,16},{16,20},{20,24},{24,28},{28,0},{1,5},{5... | collective-permute-start | bytes 1179656 | tf_op jit(solution)/shard_map/ppermute | solution.py:15
  10.3 19.2 %collective-permute-start.2 = (bf16[384,512]{1,0:T(8,128)(2,1)}, bf16[384,512]{1,0:T(8,128)(2,1)S(1)}, u32[]{:S(2)}, u32[]{:S(2)}) collective-permute-start(bf16[384,512]{1,0:T(8,128)(2,1)} %param.7), channel_id=1, source_target_pairs={{4,0},{8,4},{12,8},{16,12},{20,16},{24,20},{28,24},{0,28},{5,1},{9... | collective-permute-start | bytes 1179656 | tf_op jit(solution)/shard_map/ppermute | solution.py:18
  14.4 13.9 %collective-permute-start = (bf16[128,512]{1,0:T(8,128)(2,1)S(1)}, bf16[128,512]{1,0:T(8,128)(2,1)S(1)}, u32[]{:S(2)}, u32[]{:S(2)}) collective-permute-start(bf16[128,512]{1,0:T(8,128)(2,1)S(1)} %get-tuple-element.15), channel_id=1, source_target_pairs={{0,8},{4,12},{8,16},{12,20},{16,24},{20,28},{24,0},{28,4},{1,9},{5... | collective-permute-start | bytes 393224 | tf_op jit(solution)/shard_map/ppermute | solution.py:25
  14.4 15.1 %collective-permute-start.3 = (bf16[128,512]{1,0:T(8,128)(2,1)S(1)}, bf16[128,512]{1,0:T(8,128)(2,1)S(1)}, u32[]{:S(2)}, u32[]{:S(2)}) collective-permute-start(bf16[128,512]{1,0:T(8,128)(2,1)S(1)} %get-tuple-element.14), channel_id=1, source_target_pairs={{0,24},{4,28},{8,0},{12,4},{16,8},{20,12},{24,16},{28,20},{1,25},{... | collective-permute-start | bytes 393224 | tf_op jit(solution)/shard_map/ppermute | solution.py:25
  29.6 1.1 copy-start.1
  34.6 0.7 copy-start.3
  36.3 132.0 %reduce-scatter.2.cloned.1.call-start = ((), (), s32[]{:S(2)}) async-start(), calls=%async_computation.1 | async-start | bytes 4718592 | tf_op jit(solution)/shard_map/reduce_scatter | solution.py:73
  73.5 1.0 copy-start.4
  79.9 0.7 copy-start.5
Sparse Core Ops, SparseCore 0:
  36.4 28.6 all-gather.2
  80.0 88.2 reduce-scatter.1
